TPU v7x, 32 devices: a whole 2x2x4 slice. The times are simulated.
32 devices in a mesh: ia: 4 (over y, x), ja: 4 (over z), col: 2 (over core).
Axes of the slice: x: 2, y: 2, z: 4, core: 2. Of those that a mesh axis runs over, the one named last changes fastest.
Arguments:
- pair_rep: bfloat16 [512, 512, 128], P('ia', 'ja'), may hold values from -6 to 6
- norm_gain: float32 [128], replicated, may hold values from 0.1 to 1.9
- weights: bfloat16 [4, 128, 128], P(None, None, 'col'), may hold values from -0.5 to 0.5
- residue_mask: int32 [512], replicated, may hold values 0 or 1
- product_grad: bfloat16 [512, 128, 512], P('ia', 'col', 'ja'), may hold values from -1 to 1
Outputs:
- pair_grad: bfloat16 [512, 512, 128], P('ia', 'ja')
- weight_grads: float32 [4, 128, 128], P(None, None, 'col')
All inputs are finite; a program needn't handle non-finite values.
Results may differ from a plain program's by a relative error of at most 0.0067.
Values may be sent and summed in bfloat16 or wider, within the bound.
A program may use at most 128 MiB of HBM per device.

v0:
```python
import jax
import jax.numpy as jnp
from jax import lax
from jax.sharding import PartitionSpec as P

CLIP_LIMIT = 64.0


def gate_terms(incoming, linear, gate_pre, pair_valid):
    sigmoid_gate = jax.nn.sigmoid(gate_pre)
    through = incoming * pair_valid
    return (through * sigmoid_gate, through * linear * sigmoid_gate * (1.0 - sigmoid_gate))


def on_device(pair_rep, norm_gain, weights, residue_mask, product_grad):
    row_count = pair_rep.shape[0]
    col_count = pair_rep.shape[1]
    row_first = lax.axis_index("ia") * row_count
    col_first = lax.axis_index("ja") * col_count
    validity = residue_mask.astype(jnp.float32)
    row_valid = lax.dynamic_slice_in_dim(validity, row_first, row_count)
    col_valid = lax.dynamic_slice_in_dim(validity, col_first, col_count)
    pair_valid = row_valid[:, None, None] * col_valid[None, None, :]
    floats = pair_rep.astype(jnp.float32)
    centred = floats - jnp.mean(floats, axis=-1, keepdims=True)
    inv_std = lax.rsqrt(jnp.mean(centred * centred, axis=-1, keepdims=True) + 1e-05)
    unit_rows = centred * inv_std
    normed = (unit_rows * norm_gain).astype(jnp.bfloat16)
    projected = jnp.einsum("ikd,wdc->wick", normed, weights, preferred_element_type=jnp.float32)
    left_side = (pair_valid * jax.nn.sigmoid(projected[1]) * projected[0]).astype(jnp.bfloat16)
    right_side = (pair_valid * jax.nn.sigmoid(projected[3]) * projected[2]).astype(jnp.bfloat16)
    row_panel = lax.all_gather(product_grad, "ja", axis=2, tiled=True)
    panel_part = row_panel
    grad_left = jnp.einsum(
        "icj,jck->ick",
        panel_part,
        lax.all_gather(right_side, "ia", axis=0, tiled=True),
        preferred_element_type=jnp.float32,
    )
    panel_part = row_panel
    grad_right = lax.psum_scatter(
        jnp.einsum("icj,ick->jck", panel_part, left_side, preferred_element_type=jnp.float32),
        "ia",
        scatter_dimension=0,
        tiled=True,
    )
    lin_a, gate_a = gate_terms(grad_left, projected[0], projected[1], pair_valid)
    lin_b, gate_b = gate_terms(grad_right, projected[2], projected[3], pair_valid)
    proj_grads = jnp.stack([lin_a, gate_a, lin_b, gate_b]).astype(jnp.bfloat16)
    grad_part = jnp.einsum("ikd,wick->wdc", normed, proj_grads, preferred_element_type=jnp.float32)
    input_part = jnp.einsum(
        "wick,wdc->ikd", proj_grads, weights, preferred_element_type=jnp.float32
    )
    normed_grad = lax.psum(input_part, "col")
    scaled = normed_grad * norm_gain
    pair_grad = inv_std * (
        scaled
        - jnp.mean(scaled, axis=-1, keepdims=True)
        - unit_rows * jnp.mean(scaled * unit_rows, axis=-1, keepdims=True)
    )
    summed = lax.psum(grad_part, ("ia", "ja"))
    squares = lax.psum(jnp.sum(summed * summed), "col")
    factor = jnp.minimum(1.0, CLIP_LIMIT * lax.rsqrt(squares + 1e-06))
    weight_grads = summed * factor
    return (pair_grad.astype(jnp.bfloat16), weight_grads)


def solution(mesh):
    placed = (P("ia", "ja", None), P(), P(None, None, "col"), P(), P("ia", "col", "ja"))
    return jax.shard_map(
        on_device,
        mesh=mesh,
        in_specs=placed,
        out_specs=(P("ia", "ja", None), P(None, None, "col")),
        check_vma=False,
    )
```

profile of v0, /device:TPU:0, one launch (start us, length us, event | category | flops | bytes accessed | tf_op | source)
XLA Modules:
  0.0 660.3 jit_solution(14896707460684824877)
XLA Ops:
  7.2 0.0 copy-start
  7.2 0.0 copy-start.10
  7.2 0.0 all-gather.5.cloned.1.call-start
  7.2 4.3 copy.18
  11.5 0.0 all-gather.5.cloned.1.call-update
  11.5 0.0 all-gather.3.cloned.1.call-start
  11.6 0.0 copy-done.10
  11.6 0.0 copy-start.2
  11.6 0.1 fusion.41
  11.7 0.1 broadcast_multiply_fusion.1
  11.8 0.0 copy-start.9
  11.8 3.5 convert_reduce_fusion
  15.3 0.0 copy-done.2
  15.3 4.8 fusion.10
  20.1 0.0 copy-done
  20.2 0.0 copy-done.9
  20.2 4.7 convolution_bitcast_fusion
  24.9 0.0 copy-start.1
  24.9 5.9 copy-done.1
  30.8 2.6 multiply_convert_fusion.5
  33.4 0.0 all-gather.3.cloned.1.call-update
  33.4 0.5 reduce-scatter.2.cloned.1.call-start
  33.9 129.6 %all-gather.5.cloned.1.call-done = bf16[128,64,512]{2,0,1:T(8,128)(2,1)} async-done(((bf16[128,64,128]{2,0,1:T(8,128)(2,1)}), bf16[128,64,512]{2,0,1:T(8,128)(2,1)}) %all-gather.5.cloned.1.call-update) | async-done | bytes 8388624 | tf_op jit(solution)/shard_map/all_gather | solution.py:32
  163.5 87.5 %all-gather.3.cloned.1.call-done = bf16[512,64,128]{2,1,0:T(8,128)(2,1)} async-done(((bf16[128,64,128]{2,1,0:T(8,128)(2,1)}), bf16[512,64,128]{2,1,0:T(8,128)(2,1)}) %all-gather.3.cloned.1.call-update) | async-done | bytes 8388624 | tf_op jit(solution)/shard_map/all_gather | solution.py:37
  251.0 25.2 %fusion.11 = f32[64,128,128]{2,1,0:T(8,128)} fusion(bf16[128,64,512]{2,0,1:T(8,128)(2,1)} %all-gather.5.cloned.1.call-done, bf16[512,64,128]{2,1,0:T(8,128)(2,1)} %all-gather.3.cloned.1.call-done), kind=kOutput, calls=%fused_computation.15 | convolution fusion | flops 1073741824 | bytes 20971520 | tf_op jit(solution)/shard_map/icj,jck->ick/dot_general | solution.py:34
  276.2 5.4 copy.20
  281.6 6.8 %fusion.28 = (bf16[1,128,64,128]{3,2,1,0:T(8,128)(2,1)S(1)}, bf16[1,128,64,128]{3,2,1,0:T(8,128)(2,1)}, bf16[128,64,128]{2,1,0:T(8,128)(2,1)S(1)}) fusion(f32[64,128,128]{1,0,2:T(8,128)} %copy.20, f32[128,128]{1,0:T(8,128)S(1)} %broadcast_multiply_fusion.1, f32[4,128,64,128]{3,2,0,1:T(8,128)} %copy-done.1), kind=kLoop, calls=%fused_computation.43 | loop fusion | flops 14680064 | bytes 18939904 | tf_op jit(solution)/shard_map/stack | solution.py:49
  288.5 14.1 %fusion.32 = f32[64,128,512]{2,1,0:T(8,128)} fusion(bf16[128,64,512]{2,0,1:T(8,128)(2,1)} %all-gather.5.cloned.1.call-done, bf16[128,64,128]{2,1,0:T(8,128)(2,1)S(1)} %get-tuple-element.8), kind=kOutput, calls=%fused_computation.47 | convolution fusion | flops 1073741824 | bytes 27262976 | tf_op jit(solution)/shard_map/icj,ick->jck/dot_general | solution.py:42
  302.6 16.6 %copy.23 = f32[64,128,512]{1,0,2:T(8,128)} copy(f32[64,128,512]{2,1,0:T(8,128)} %fusion.32) | data formatting | bytes 33554432 | tf_op jit(solution)/shard_map/icj,ick->jck/dot_general | solution.py:42
  319.2 0.0 reduce-scatter.2.cloned.1.call-update
  319.2 0.0 all-reduce.5.cloned.1.call-start
  319.2 153.8 %reduce-scatter.2.cloned.1.call-done = f32[128,64,128]{2,1,0:T(8,128)} async-done(((f32[512,64,128]{2,1,0:T(8,128)}), f32[128,64,128]{2,1,0:T(8,128)}) %reduce-scatter.2.cloned.1.call-update) | async-done | bytes 4194320 | tf_op jit(solution)/shard_map/reduce_scatter | solution.py:41
  473.1 6.0 fusion.30
  479.1 0.0 copy-start.7
  479.2 1.3 copy-done.7
  480.4 0.7 copy-done.8
  481.1 5.4 fusion.34
  486.5 0.0 all-reduce.5.cloned.1.call-update
  486.6 0.0 all-reduce.3.cloned.1.call-start
  486.6 6.5 convolution_bitcast_fusion.1
  493.1 0.0 all-reduce.3.cloned.1.call-update
  493.1 99.0 %all-reduce.5.cloned.1.call-done = f32[4,128,64]{1,2,0:T(8,128)} async-done(((f32[4,128,64]{1,2,0:T(8,128)}), f32[4,128,64]{1,2,0:T(8,128)}) %all-reduce.5.cloned.1.call-update) | async-done | bytes 131088 | tf_op jit(solution)/shard_map/psum | solution.py:61
  592.1 1.5 multiply_reduce_fusion.1
  593.7 3.1 psum.23
  597.4 1.6 broadcast_multiply_fusion
  599.0 32.2 %all-reduce.3.cloned.1.call-done = f32[128,128,128]{2,1,0:T(8,128)} async-done(((f32[128,128,128]{2,1,0:T(8,128)}), f32[128,128,128]{2,1,0:T(8,128)}) %all-reduce.3.cloned.1.call-update) | async-done | bytes 8388624 | tf_op jit(solution)/shard_map/psum | solution.py:54
  631.2 11.6 %multiply_reduce_fusion = (f32[128,128]{1,0:T(8,128)S(1)}, f32[128,128]{1,0:T(8,128)S(1)}) fusion(f32[128,128,128]{2,1,0:T(8,128)} %all-reduce.3.cloned.1.call-done, f32[128]{0:T(128)S(1)} %copy-done.9, f32[128,128]{1,0:T(8,128)S(1)} %add_rsqrt_fusion, f32[128,128]{1,0:T(8,128)S(1)} %broadcast_multiply_fusion.4, bf16[128,128,128]{2,1,0:T(8,128)(2,1)} %param.5), kind=kLoop, calls=%fused_computation.17 | loop fusion | flops 14647296 | bytes 12845568 | tf_op jit(solution)/shard_map/reduce_sum | solution.py:58
  642.8 10.7 %fusion.9 = bf16[128,128,128]{2,1,0:T(8,128)(2,1)} fusion(bf16[128,128,128]{2,1,0:T(8,128)(2,1)S(1)} %copy-done.4, f32[128,128,128]{2,1,0:T(8,128)S(1)} %copy-done.5, f32[128,128]{1,0:T(8,128)S(1)} %get-tuple-element.11, f32[128,128]{1,0:T(8,128)S(1)} %get-tuple-element.12, f32[128]{0:T(128)S(1)} %copy-done.9, f32[128,128]{1,0:T(8,128)S(1)} %add_rsqrt_fusion, ...), kind=kLoop, calls=%fused_computation.12 | loop fusion | flops 18874368 | bytes 17039872 | tf_op jit(solution)/shard_map/convert_element_type | solution.py:65
  (13 shorter events, 0.1 us)
Async XLA Ops:
  7.2 13.0 %copy-start = (bf16[4,128,64]{1,2,0:T(8,128)(2,1)S(1)}, bf16[4,128,64]{1,2,0:T(8,128)(2,1)}, u32[]{:S(2)}) copy-start(bf16[4,128,64]{1,2,0:T(8,128)(2,1)} %param.7) | copy-start | bytes 196612
  7.2 4.4 copy-start.10
  7.2 156.3 %all-gather.5.cloned.1.call-start = ((), (), s32[]{:S(2)}) async-start(), calls=%async_computation.2 | async-start | bytes 10485760 | tf_op jit(solution)/shard_map/all_gather | solution.py:32
  11.5 239.5 %all-gather.3.cloned.1.call-start = ((), (), s32[]{:S(2)}) async-start(), calls=%async_computation.1 | async-start | bytes 10485760 | tf_op jit(solution)/shard_map/all_gather | solution.py:37
  11.6 3.7 copy-start.2
  11.8 8.4 %copy-start.9 = (f32[128]{0:T(128)S(1)}, f32[128]{0:T(128)}, u32[]{:S(2)}) copy-start(f32[128]{0:T(128)} %param.6) | copy-start | bytes 1540
  24.9 5.9 copy-start.1
  33.4 439.6 %reduce-scatter.2.cloned.1.call-start = ((), (), s32[]{:S(2)}) async-start(), calls=%async_computation.3 | async-start | bytes 20971520 | tf_op jit(solution)/shard_map/reduce_scatter | solution.py:41
  319.2 272.9 %all-reduce.5.cloned.1.call-start = ((), (), s32[]{:S(2)}) async-start(), calls=%async_computation.5 | async-start | bytes 262144 | tf_op jit(solution)/shard_map/psum | solution.py:61
  473.1 8.0 %copy-start.3 = (bf16[128,128,128]{2,1,0:T(8,128)(2,1)S(1)}, bf16[128,128,128]{2,1,0:T(8,128)(2,1)}, u32[]{:S(2)}) copy-start(bf16[128,128,128]{2,1,0:T(8,128)(2,1)} %param.5) | copy-start | bytes 12582916
  473.1 8.0 %copy-start.6 = (bf16[1,128,64,128]{3,2,1,0:T(8,128)(2,1)S(1)}, bf16[1,128,64,128]{3,2,1,0:T(8,128)(2,1)}, u32[]{:S(2)}) copy-start(bf16[1,128,64,128]{3,2,1,0:T(8,128)(2,1)} %get-tuple-element.5) | copy-start | bytes 6291460
  479.1 1.3 copy-start.7
  479.1 2.0 copy-start.8
  486.6 144.6 %all-reduce.3.cloned.1.call-start = ((), (), s32[]{:S(2)}) async-start(), calls=%async_computation.4 | async-start | bytes 16777216 | tf_op jit(solution)/shard_map/psum | solution.py:54
  631.2 11.6 %copy-start.4 = (bf16[128,128,128]{2,1,0:T(8,128)(2,1)S(1)}, bf16[128,128,128]{2,1,0:T(8,128)(2,1)}, u32[]{:S(2)}) copy-start(bf16[128,128,128]{2,1,0:T(8,128)(2,1)} %param.5) | copy-start | bytes 12582916
  631.2 11.6 %copy-start.5 = (f32[128,128,128]{2,1,0:T(8,128)S(1)}, f32[128,128,128]{2,1,0:T(8,128)}, u32[]{:S(2)}) copy-start(f32[128,128,128]{2,1,0:T(8,128)} %all-reduce.3.cloned.1.call-done) | copy-start | bytes 25165828
Sparse Core Ops, SparseCore 0:
  11.6 151.8 all-gather.4
  165.4 85.6 all-gather.2
  319.3 153.7 reduce-scatter.1
  486.7 105.3 all-reduce.4
  594.4 36.6 all-reduce.2
where the time goes:
time: 668 us; the launch traced here: 660 us
  waiting for transfers between devices  502 us (75%)
  matrix products  55.9 us (8%)
  other arithmetic  49.3 us (7%)
  local copies, waits for them, and re-layouts  34.2 us (5%)
  between operations  14.9 us (2%)
    reduce_scatter x1, waiting for transfers between devices, on_device(): lax.psum_scatter(jnp.einsum('icj,ick->jck', panel_part, left_side, prefer...  154 us
    all_gather x1, waiting for transfers between devices, on_device(): row_panel = lax.all_gather(product_grad, 'ja', axis=2, tiled=True)  130 us
    psum x1, waiting for transfers between devices, on_device(): summed = lax.psum(grad_part, ('ia', 'ja'))  99 us
    all_gather x1, waiting for transfers between devices, on_device(): lax.all_gather(right_side, 'ia', axis=0, tiled=True)  87.5 us
    psum x1, waiting for transfers between devices, on_device(): normed_grad = lax.psum(input_part, 'col')  32.2 us
    dot_general x1, matrix products, on_device(): jnp.einsum('icj,jck->ick', panel_part, lax.all_gather(right_side, 'ia', a...  25.2 us
    dot_general x1, local copies, waits for them, and re-layouts, on_device(): jnp.einsum('icj,ick->jck', panel_part, left_side, preferred_element_type=...  16.6 us
    dot_general x1, matrix products, on_device(): jnp.einsum('icj,ick->jck', panel_part, left_side, preferred_element_type=...  14.1 us
  transfers between devices with their start and end apart: 5, of which 5 were waited for; matrix products, arithmetic and copies ran while one was open for 4% of the time, Pallas kernels for 0%

commit v1 on v0

--- a/solution.py
+++ b/solution.py
@@ -31,12 +31,26 @@
     right_side = (pair_valid * jax.nn.sigmoid(projected[3]) * projected[2]).astype(jnp.bfloat16)
     row_panel = lax.all_gather(product_grad, "ja", axis=2, tiled=True)
     panel_part = row_panel
+    count, here = (lax.axis_size("ia"), lax.axis_index("ia"))
+    backward = [(i, (i - 1) % count) for i in range(count)]
+    span = right_side.shape[0]
+    block = right_side
     grad_left = jnp.einsum(
         "icj,jck->ick",
-        panel_part,
-        lax.all_gather(right_side, "ia", axis=0, tiled=True),
+        lax.dynamic_slice_in_dim(panel_part, here * span, block.shape[0], axis=2),
+        block,
         preferred_element_type=jnp.float32,
     )
+    for step in range(1, count):
+        block = lax.ppermute(block, "ia", backward)
+        grad_left = grad_left + jnp.einsum(
+            "icj,jck->ick",
+            lax.dynamic_slice_in_dim(
+                panel_part, (here + step) % count * span, block.shape[0], axis=2
+            ),
+            block,
+            preferred_element_type=jnp.float32,
+        )
     panel_part = row_panel
     grad_right = lax.psum_scatter(
         jnp.einsum("icj,ick->jck", panel_part, left_side, preferred_element_type=jnp.float32),

time: 668 us -> 623 us (0.933)
  waiting for transfers between devices: 502 us -> 419 us
  local copies, waits for them, and re-layouts: 34.2 us -> 52.5 us
  starting transfers between devices: 0.67 us -> 11.4 us
  other arithmetic: 49.3 us -> 57.8 us
    ppermute x0 -> x3, waiting for transfers between devices: none -> 132 us  [on_device(): block = lax.ppermute(block, 'ia', backward)]
    all_gather x1, waiting for transfers between devices: 130 us -> 0.01 us  [on_device(): row_panel = lax.all_gather(product_grad, 'ja', axis=2, tiled=True)]
    all_gather x1 -> x0, waiting for transfers between devices: 87.5 us -> none  [on_device(): lax.all_gather(right_side, 'ia', axis=0, tiled=True)]
    dot_general x1 -> x4, local copies, waits for them, and re-layouts: 5.42 us -> 21.6 us  [the longest x3 16.2 us: on_device(): jnp.einsum('icj,jck->ick', lax.dynamic_slice_in_dim(panel_part, (here + s...]
    ppermute x0 -> x3, starting transfers between devices: none -> 11.3 us  [on_device(): block = lax.ppermute(block, 'ia', backward)]
    another operation x2, other arithmetic: 12.9 us -> 22.7 us  [on_device(): proj_grads = jnp.stack([lin_a, gate_a, lin_b, gate_b]).astype(jnp.bfloat16)]
    unnamed x23 -> x25, local copies, waits for them, and re-layouts: 12.2 us -> 14.2 us
    dot_general x1 -> x4, matrix products: 25.2 us -> 24.7 us  [the longest x3 19 us: on_device(): jnp.einsum('icj,jck->ick', lax.dynamic_slice_in_dim(panel_part, (here + s...]
  transfers between devices with their start and end apart: 5 -> 7, of which waited for: 5 -> 6; matrix products, arithmetic and copies ran while one was open for 4% -> 4% of each run, Pallas kernels for 0% -> 0%
where the time goes in v1:
time: 623 us; the launch traced here: 615 us
  waiting for transfers between devices  419 us (67%)
  other arithmetic  57.8 us (9%)
  matrix products  55.7 us (9%)
  local copies, waits for them, and re-layouts  52.5 us (8%)
  between operations  14.9 us (2%)
  starting transfers between devices  11.4 us (2%)
    reduce_scatter x1, waiting for transfers between devices, on_device(): lax.psum_scatter(jnp.einsum('icj,ick->jck', panel_part, left_side, prefer...  156 us
    ppermute x3, waiting for transfers between devices, on_device(): block = lax.ppermute(block, 'ia', backward)  132 us
    psum x1, waiting for transfers between devices, on_device(): summed = lax.psum(grad_part, ('ia', 'ja'))  98.7 us
    psum x1, waiting for transfers between devices, on_device(): normed_grad = lax.psum(input_part, 'col')  32.2 us
    another operation x2, other arithmetic, on_device(): proj_grads = jnp.stack([lin_a, gate_a, lin_b, gate_b]).astype(jnp.bfloat16)  22.7 us
    dot_general x3, matrix products, on_device(): jnp.einsum('icj,jck->ick', lax.dynamic_slice_in_dim(panel_part, (here + s...  19 us
    dot_general x1, local copies, waits for them, and re-layouts, on_device(): jnp.einsum('icj,ick->jck', panel_part, left_side, preferred_element_type=...  16.5 us
    dot_general x3, local copies, waits for them, and re-layouts, on_device(): jnp.einsum('icj,jck->ick', lax.dynamic_slice_in_dim(panel_part, (here + s...  16.2 us
  transfers between devices with their start and end apart: 7, of which 6 were waited for; matrix products, arithmetic and copies ran while one was open for 4% of the time, Pallas kernels for 0%

profile of v1, /device:TPU:0, one launch (start us, length us, event | category | flops | bytes accessed | tf_op | source)
XLA Modules:
  0.0 614.7 jit_solution(14509186678330371873)
XLA Ops:
  7.2 0.0 all-gather.2.cloned.1.call-start
  7.2 4.3 copy.9
  11.5 0.0 all-gather.2.cloned.1.call-update
  11.5 0.0 reduce-scatter.2.cloned.1.call-start
  11.6 0.1 fusion.55
  11.7 0.1 broadcast_multiply_fusion.1
  11.8 3.5 convert_reduce_fusion
  15.3 4.8 fusion.10
  20.2 4.7 convolution_bitcast_fusion
  24.9 5.9 copy-done.1
  30.8 1.3 multiply_convert_fusion.5
  32.1 4.0 collective-permute-start
  36.0 44.9 %collective-permute-done = bf16[128,64,128]{2,1,0:T(8,128)(2,1)S(1)} collective-permute-done((bf16[128,64,128]{2,1,0:T(8,128)(2,1)S(1)}, bf16[128,64,128]{2,1,0:T(8,128)(2,1)S(1)}, u32[]{:S(2)}, u32[]{:S(2)}) %collective-permute-start) | collective-permute-done | bytes 2097184 | tf_op jit(solution)/shard_map/ppermute | solution.py:45
  80.9 1.4 copy-done.6
  82.3 3.4 collective-permute-start.1
  85.7 44.0 %collective-permute-done.1 = bf16[128,64,128]{2,1,0:T(8,128)(2,1)} collective-permute-done((bf16[128,64,128]{2,1,0:T(8,128)(2,1)S(1)}, bf16[128,64,128]{2,1,0:T(8,128)(2,1)}, u32[]{:S(2)}, u32[]{:S(2)}) %collective-permute-start.1) | collective-permute-done | bytes 2097184 | tf_op jit(solution)/shard_map/ppermute | solution.py:45
  129.7 3.9 collective-permute-start.2
  133.6 43.5 %collective-permute-done.2 = bf16[128,64,128]{2,1,0:T(8,128)(2,1)} collective-permute-done((bf16[128,64,128]{2,1,0:T(8,128)(2,1)}, bf16[128,64,128]{2,1,0:T(8,128)(2,1)}, u32[]{:S(2)}, u32[]{:S(2)}) %collective-permute-start.2) | collective-permute-done | bytes 2097184 | tf_op jit(solution)/shard_map/ppermute | solution.py:45
  177.1 6.3 %fusion.32 = f32[64,128,128]{2,1,0:T(8,128)} fusion(bf16[128,64,128]{2,1,0:T(8,128)(2,1)} %collective-permute-done.2, bf16[128,64,512]{2,0,1:T(8,128)(2,1)} %all-gather.2.cloned.1.call-done, s32[]{:T(128)S(6)} %select_n.38), kind=kOutput, calls=%fused_computation.47 | convolution fusion | flops 268435456 | bytes 8388612 | tf_op jit(solution)/shard_map/icj,jck->ick/dot_general | solution.py:46
  183.4 5.4 copy.17
  188.8 6.3 %fusion.34 = f32[64,128,128]{2,1,0:T(8,128)} fusion(bf16[128,64,128]{2,1,0:T(8,128)(2,1)} %collective-permute-done.1, bf16[128,64,512]{2,0,1:T(8,128)(2,1)} %all-gather.2.cloned.1.call-done, s32[]{:T(128)S(6)} %select_n.36), kind=kOutput, calls=%fused_computation.49 | convolution fusion | flops 268435456 | bytes 8388612 | tf_op jit(solution)/shard_map/icj,jck->ick/dot_general | solution.py:46
  195.2 5.4 copy.15
  200.6 6.3 %fusion.36 = f32[64,128,128]{2,1,0:T(8,128)} fusion(bf16[128,64,128]{2,1,0:T(8,128)(2,1)} %copy-done.6, bf16[128,64,512]{2,0,1:T(8,128)(2,1)} %all-gather.2.cloned.1.call-done, s32[]{:T(128)S(6)} %select_n.34), kind=kOutput, calls=%fused_computation.51 | convolution fusion | flops 268435456 | bytes 8388612 | tf_op jit(solution)/shard_map/icj,jck->ick/dot_general | solution.py:46
  206.9 5.4 copy.13
  212.3 5.7 fusion.38
  218.0 5.4 copy.12
  223.4 12.3 %fusion.26 = (bf16[1,128,64,128]{3,2,1,0:T(8,128)(2,1)S(1)}, f32[128,64,128]{2,1,0:T(8,128)}, bf16[128,64,128]{2,1,0:T(8,128)(2,1)S(1)}) fusion(f32[4,128,64,128]{3,2,0,1:T(8,128)} %copy-done.1, f32[128,128]{1,0:T(8,128)S(1)} %broadcast_multiply_fusion.1, f32[64,128,128]{1,0,2:T(8,128)} %copy.17, f32[64,128,128]{1,0,2:T(8,128)} %copy.15, ...), kind=kLoop, calls=%fused_computation.41 | loop fusion | flops 12582912 | bytes 33619968 | tf_op jit(solution)/shard_map/stack | solution.py:63
  235.7 14.1 %fusion.30 = f32[64,128,512]{2,1,0:T(8,128)} fusion(bf16[128,64,512]{2,0,1:T(8,128)(2,1)} %all-gather.2.cloned.1.call-done, bf16[128,64,128]{2,1,0:T(8,128)(2,1)S(1)} %get-tuple-element.8), kind=kOutput, calls=%fused_computation.45 | convolution fusion | flops 1073741824 | bytes 27262976 | tf_op jit(solution)/shard_map/icj,ick->jck/dot_general | solution.py:56
  249.9 16.5 %copy.20 = f32[64,128,512]{1,0,2:T(8,128)} copy(f32[64,128,512]{2,1,0:T(8,128)} %fusion.30) | data formatting | bytes 33554432 | tf_op jit(solution)/shard_map/icj,ick->jck/dot_general | solution.py:56
  266.4 0.0 reduce-scatter.2.cloned.1.call-update
  266.4 0.0 all-reduce.5.cloned.1.call-start
  266.5 156.0 %reduce-scatter.2.cloned.1.call-done = f32[128,64,128]{2,1,0:T(8,128)} async-done(((f32[512,64,128]{2,1,0:T(8,128)}), f32[128,64,128]{2,1,0:T(8,128)}) %reduce-scatter.2.cloned.1.call-update) | async-done | bytes 4194320 | tf_op jit(solution)/shard_map/reduce_scatter | solution.py:55
  422.5 10.3 %fusion.28 = (bf16[1,128,64,128]{3,2,1,0:T(8,128)(2,1)S(1)}, bf16[1,128,64,128]{3,2,1,0:T(8,128)(2,1)S(1)}, bf16[1,128,64,128]{3,2,1,0:T(8,128)(2,1)S(1)}) fusion(f32[128,64,128]{2,1,0:T(8,128)} %reduce-scatter.2.cloned.1.call-done, f32[128,128]{1,0:T(8,128)S(1)} %broadcast_multiply_fusion.1, f32[4,128,64,128]{3,2,0,1:T(8,128)} %copy-done.1, ...), kind=kLoop, calls=%fused_computation.43 | loop fusion | flops 19922944 | bytes 31522816 | tf_op jit(solution)/shard_map/stack | solution.py:63
  432.9 1.3 copy-done.7
  434.2 0.6 copy-done.8
  434.8 0.7 copy-done.9
  435.5 5.4 fusion.44
  440.9 0.0 all-reduce.5.cloned.1.call-update
  441.0 0.0 all-reduce.3.cloned.1.call-start
  441.0 6.7 %convolution_bitcast_fusion.1 = f32[128,128,128]{2,1,0:T(8,128)} fusion(bf16[1,128,64,128]{3,2,1,0:T(8,128)(2,1)} %copy-done.8, bf16[1,128,64,128]{3,2,1,0:T(8,128)(2,1)} %copy-done.7, bf16[1,128,64,128]{3,2,1,0:T(8,128)(2,1)} %copy-done.9, bf16[1,128,64,128]{3,2,1,0:T(8,128)(2,1)S(1)} %get-tuple-element.4, bf16[4,128,64]{1,2,0:T(8,128)(2,1)S(1)} %copy-done), kind=kOutput, calls=%fused_computation.40 | convolution fusion | flops 1086324736 | bytes 16842752 | tf_op jit(solution)/shard_map/wick,wdc->ikd/dot_general | solution.py:65
  447.8 0.0 all-reduce.3.cloned.1.call-update
  447.8 98.7 %all-reduce.5.cloned.1.call-done = f32[4,128,64]{1,2,0:T(8,128)} async-done(((f32[4,128,64]{1,2,0:T(8,128)}), f32[4,128,64]{1,2,0:T(8,128)}) %all-reduce.5.cloned.1.call-update) | async-done | bytes 131088 | tf_op jit(solution)/shard_map/psum | solution.py:75
  546.5 1.5 multiply_reduce_fusion.1
  548.1 3.1 psum.23
  551.8 1.6 broadcast_multiply_fusion
  553.4 32.2 %all-reduce.3.cloned.1.call-done = f32[128,128,128]{2,1,0:T(8,128)} async-done(((f32[128,128,128]{2,1,0:T(8,128)}), f32[128,128,128]{2,1,0:T(8,128)}) %all-reduce.3.cloned.1.call-update) | async-done | bytes 8388624 | tf_op jit(solution)/shard_map/psum | solution.py:68
  585.6 11.6 %multiply_reduce_fusion = (f32[128,128]{1,0:T(8,128)S(1)}, f32[128,128]{1,0:T(8,128)S(1)}) fusion(f32[128,128,128]{2,1,0:T(8,128)} %all-reduce.3.cloned.1.call-done, f32[128]{0:T(128)S(1)} %copy-done.10, f32[128,128]{1,0:T(8,128)S(1)} %add_rsqrt_fusion, f32[128,128]{1,0:T(8,128)S(1)} %broadcast_multiply_fusion.4, bf16[128,128,128]{2,1,0:T(8,128)(2,1)} %param.5), kind=kLoop, calls=%fused_computation.15 | loop fusion | flops 14647296 | bytes 12845568 | tf_op jit(solution)/shard_map/reduce_sum | solution.py:72
  597.2 10.7 %fusion.9 = bf16[128,128,128]{2,1,0:T(8,128)(2,1)} fusion(bf16[128,128,128]{2,1,0:T(8,128)(2,1)S(1)} %copy-done.4, f32[128,128,128]{2,1,0:T(8,128)S(1)} %copy-done.5, f32[128,128]{1,0:T(8,128)S(1)} %get-tuple-element.12, f32[128,128]{1,0:T(8,128)S(1)} %get-tuple-element.13, f32[128]{0:T(128)S(1)} %copy-done.10, f32[128,128]{1,0:T(8,128)S(1)} %add_rsqrt_fusion, ...), kind=kLoop, calls=%fused_computation.12 | loop fusion | flops 18874368 | bytes 17039872 | tf_op jit(solution)/shard_map/convert_element_type | solution.py:79
  (24 shorter events, 0.1 us)
Async XLA Ops:
  7.2 13.0 %copy-start = (bf16[4,128,64]{1,2,0:T(8,128)(2,1)S(1)}, bf16[4,128,64]{1,2,0:T(8,128)(2,1)}, u32[]{:S(2)}) copy-start(bf16[4,128,64]{1,2,0:T(8,128)(2,1)} %param.7) | copy-start | bytes 196612
  7.2 4.4 copy-start.11
  7.2 169.9 %all-gather.2.cloned.1.call-start = ((), (), s32[]{:S(2)}) async-start(), calls=%async_computation.1 | async-start | bytes 10485760 | tf_op jit(solution)/shard_map/all_gather | solution.py:32
  11.5 411.0 %reduce-scatter.2.cloned.1.call-start = ((), (), s32[]{:S(2)}) async-start(), calls=%async_computation.2 | async-start | bytes 20971520 | tf_op jit(solution)/shard_map/reduce_scatter | solution.py:55
  11.6 3.7 copy-start.2
  11.8 8.4 %copy-start.10 = (f32[128]{0:T(128)S(1)}, f32[128]{0:T(128)}, u32[]{:S(2)}) copy-start(f32[128]{0:T(128)} %param.6) | copy-start | bytes 1540
  24.9 5.9 copy-start.1
  32.1 48.9 %collective-permute-start = (bf16[128,64,128]{2,1,0:T(8,128)(2,1)S(1)}, bf16[128,64,128]{2,1,0:T(8,128)(2,1)S(1)}, u32[]{:S(2)}, u32[]{:S(2)}) collective-permute-start(bf16[128,64,128]{2,1,0:T(8,128)(2,1)S(1)} %multiply_convert_fusion.5), channel_id=1, source_target_pairs={{0,24},{8,0},{16,8},{24,16},{1,25},{9,1},{17,9},{25,17},{2,26},{10... | collective-permute-start | bytes 6291464 | tf_op jit(solution)/shard_map/ppermute | solution.py:45
  80.9 1.4 copy-start.6
  82.3 47.4 %collective-permute-start.1 = (bf16[128,64,128]{2,1,0:T(8,128)(2,1)S(1)}, bf16[128,64,128]{2,1,0:T(8,128)(2,1)}, u32[]{:S(2)}, u32[]{:S(2)}) collective-permute-start(bf16[128,64,128]{2,1,0:T(8,128)(2,1)S(1)} %collective-permute-done), channel_id=1, source_target_pairs={{0,24},{8,0},{16,8},{24,16},{1,25},{9,1},{17,9},{25,17},{2,26},{10... | collective-permute-start | bytes 6291464 | tf_op jit(solution)/shard_map/ppermute | solution.py:45
  129.7 47.4 %collective-permute-start.2 = (bf16[128,64,128]{2,1,0:T(8,128)(2,1)}, bf16[128,64,128]{2,1,0:T(8,128)(2,1)}, u32[]{:S(2)}, u32[]{:S(2)}) collective-permute-start(bf16[128,64,128]{2,1,0:T(8,128)(2,1)} %collective-permute-done.1), channel_id=1, source_target_pairs={{0,24},{8,0},{16,8},{24,16},{1,25},{9,1},{17,9},{25,17},{2,26},{10... | collective-permute-start | bytes 6291464 | tf_op jit(solution)/shard_map/ppermute | solution.py:45
  266.4 280.1 %all-reduce.5.cloned.1.call-start = ((), (), s32[]{:S(2)}) async-start(), calls=%async_computation.4 | async-start | bytes 262144 | tf_op jit(solution)/shard_map/psum | solution.py:75
  422.5 13.1 %copy-start.3 = (bf16[128,128,128]{2,1,0:T(8,128)(2,1)S(1)}, bf16[128,128,128]{2,1,0:T(8,128)(2,1)}, u32[]{:S(2)}) copy-start(bf16[128,128,128]{2,1,0:T(8,128)(2,1)} %param.5) | copy-start | bytes 12582916
  432.8 1.4 copy-start.7
  432.8 2.0 copy-start.8
  432.9 2.7 copy-start.9
  441.0 144.6 %all-reduce.3.cloned.1.call-start = ((), (), s32[]{:S(2)}) async-start(), calls=%async_computation.3 | async-start | bytes 16777216 | tf_op jit(solution)/shard_map/psum | solution.py:68
  585.6 11.6 %copy-start.4 = (bf16[128,128,128]{2,1,0:T(8,128)(2,1)S(1)}, bf16[128,128,128]{2,1,0:T(8,128)(2,1)}, u32[]{:S(2)}) copy-start(bf16[128,128,128]{2,1,0:T(8,128)(2,1)} %param.5) | copy-start | bytes 12582916
  585.6 11.6 %copy-start.5 = (f32[128,128,128]{2,1,0:T(8,128)S(1)}, f32[128,128,128]{2,1,0:T(8,128)}, u32[]{:S(2)}) copy-start(f32[128,128,128]{2,1,0:T(8,128)} %all-reduce.3.cloned.1.call-done) | copy-start | bytes 25165828
Sparse Core Ops, SparseCore 0:
  11.6 151.8 all-gather.1
  266.5 155.8 reduce-scatter.1
  441.1 105.3 all-reduce.4
  548.8 36.6 all-reduce.2
